TPU v7x, 32 devices: a whole 2x2x4 slice. The times are simulated.
32 devices in a mesh: row: 8 (over z, y), col: 4 (over x, core).
Axes of the slice: x: 2, y: 2, z: 4, core: 2. Of those that a mesh axis runs over, the one named last changes fastest.
Arguments:
- spectrum: float32 [2, 4096, 2048], P(None, 'row', 'col'), may hold values from -6 to 6
- pupil: float32 [2, 512, 512], replicated, may hold values from -4.2 to 4.2
- amplitudes: float32 [8, 4, 1, 512, 512], P('row', 'col'), may hold values from 0.1 to 3
- offsets: int32 [8, 4, 1, 2], P('row', 'col'), may hold values from 0 to 511, as said below
- counts: int32 [8, 4], P('row', 'col'), may hold values from 1 to 1, as said below
Outputs:
- recovered: float32 [2, 4096, 2048], P(None, 'row', 'col')
Inputs may be any that keep to these rules, and one draw needn't show every extreme that they name: `offsets`: offsets are corners inside the tile: the row below 512, the column below 512. `counts`: some device has all 1 slots live.
All inputs are finite; a program needn't handle non-finite values.
Results may differ from a plain program's by a relative error of at most 0.012.
Values sent between devices are 32-bit elements; how exact they have to be, the bound alone decides.
A program may use at most 128 MiB of HBM per device.

v0:
```python
import math

import jax
import jax.numpy as jnp
from jax import lax
from jax.sharding import PartitionSpec as P

SWEEPS = 2


step_size = 0.5
floor_value = 0.05


def shifted(value, axis, steps):
    count = lax.axis_size(axis)
    leading, last = (max(0, -steps), min(count, count - steps))
    return lax.ppermute(value, axis, [(source, source + steps) for source in range(leading, last)])


def dft_tables(width):
    index = jnp.arange(width, dtype=jnp.int32)
    phase = index[:, None] * index[None, :] % width
    angle = phase.astype(jnp.float32) * (2.0 * math.pi / width)
    scale = 1.0 / math.sqrt(width)
    return (
        (jnp.cos(angle) * scale).astype(jnp.bfloat16),
        (jnp.sin(angle) * scale).astype(jnp.bfloat16),
    )


def transform(real, imag, cosine, sine, sign):
    real = real.astype(jnp.bfloat16)
    imag = imag.astype(jnp.bfloat16)

    def right(a, b):
        return jnp.einsum("swk,kj->swj", a, b, preferred_element_type=jnp.float32)

    def left(b, a):
        return jnp.einsum("ik,skj->sij", b, a, preferred_element_type=jnp.float32)

    first_real = (right(real, cosine) - sign * right(imag, sine)).astype(jnp.bfloat16)
    first_imag = (right(imag, cosine) + sign * right(real, sine)).astype(jnp.bfloat16)
    out_real = left(cosine, first_real) - sign * left(sine, first_imag)
    out_imag = left(cosine, first_imag) + sign * left(sine, first_real)
    return (out_real, out_imag)


def slot_gradient(windows, pupil, amps, live, cosine, sine):
    pupil_real = pupil[0][None]
    pupil_imag = pupil[1][None]
    window_real = windows[:, 0]
    window_imag = windows[:, 1]
    field_real = window_real * pupil_real - window_imag * pupil_imag
    field_imag = window_real * pupil_imag + window_imag * pupil_real
    wave_real, wave_imag = transform(field_real, field_imag, cosine, sine, 1.0)
    magnitude = jnp.sqrt(wave_real * wave_real + wave_imag * wave_imag)
    keep = 1.0 - amps / jnp.maximum(magnitude, floor_value)
    back_real, back_imag = transform(wave_real * keep, wave_imag * keep, cosine, sine, -1.0)
    mask = live[:, None, None]
    grad_real = (back_real * pupil_real + back_imag * pupil_imag) * mask
    grad_imag = (back_imag * pupil_real - back_real * pupil_imag) * mask
    return jnp.stack([grad_real, grad_imag], axis=1)


def extend(tile):
    below = shifted(tile, "row", -1)
    tall = jnp.concatenate([tile, below], axis=1)
    right = shifted(tall, "col", -1)
    return jnp.concatenate([tall, right], axis=2)


def fold_back(region, rows, cols, width):
    right = shifted(region[:, :, cols:], "col", 1)
    left_part = jnp.concatenate([region[:, :, :width] + right, region[:, :, width:cols]], axis=2)
    bottom = shifted(left_part[:, rows:, :], "row", 1)
    return jnp.concatenate([left_part[:, :width, :] + bottom, left_part[:, width:rows, :]], axis=1)


def add_piece(region, piece, place):
    zero = jnp.zeros((), jnp.int32)
    start = (zero, place[0], place[1])
    return lax.dynamic_update_slice(region, piece, start)


def on_device(spectrum, pupil, amplitudes, offsets, counts):
    width = pupil.shape[1]
    rows = spectrum.shape[1]
    cols = spectrum.shape[2]
    amps = amplitudes[0, 0]
    places = offsets[0, 0]
    live_count = counts[0, 0]
    slots = amps.shape[0]
    cosine, sine = dft_tables(width)
    live = (jnp.arange(slots, dtype=jnp.int32) < live_count).astype(jnp.float32)
    zero = jnp.zeros((), jnp.int32)
    for sweep in range(SWEEPS):
        region = extend(spectrum)
        empty = jnp.zeros_like(region)

        def cut_window(place):
            return lax.dynamic_slice(region, (zero, place[0], place[1]), (2, width, width))

        windows = jax.vmap(cut_window)(places)
        pieces = slot_gradient(windows, pupil, amps, live, cosine, sine)
        gathered = empty
        gathered = add_piece(gathered, pieces[0], places[0])
        gradient = fold_back(gathered, rows, cols, width)
        spectrum = spectrum - step_size * gradient
    return spectrum


def solution(mesh):
    in_specs = (
        P(None, "row", "col"),
        P(),
        P("row", "col", None, None, None),
        P("row", "col", None, None),
        P("row", "col"),
    )
    out_specs = P(None, "row", "col")
    return jax.shard_map(
        on_device, mesh=mesh, in_specs=in_specs, out_specs=out_specs, check_vma=False
    )
```

profile of v0, /device:TPU:25, one launch (start us, length us, event | category | flops | bytes accessed | tf_op | source)
XLA Modules:
  0.0 584.4 jit_solution(12819617424710149800)
XLA Ops:
  6.1 42.5 %collective-permute-done = f32[2,512,512]{2,1,0:T(8,128)S(1)} collective-permute-done((f32[2,512,512]{2,1,0:T(8,128)}, f32[2,512,512]{2,1,0:T(8,128)S(1)}, u32[]{:S(2)}, u32[]{:S(2)}) %collective-permute-start) | collective-permute-done | bytes 2097184 | tf_op jit(solution)/shard_map/ppermute | solution.py:18
  50.2 3.4 collective-permute-start.1
  66.6 34.6 %collective-permute-done.1 = f32[2,1024,512]{2,1,0:T(8,128)} collective-permute-done((f32[2,1024,512]{2,1,0:T(8,128)}, f32[2,1024,512]{2,1,0:T(8,128)}, u32[]{:S(2)}, u32[]{:S(2)}) %collective-permute-start.1) | collective-permute-done | bytes 4194336 | tf_op jit(solution)/shard_map/ppermute | solution.py:18
  101.2 4.2 fusion.2
  105.4 3.4 copy.6
  110.9 5.0 fusion.64
  115.9 5.0 fusion.66
  121.0 5.1 fusion.28
  126.0 5.1 fusion.27
  131.1 5.0 fusion.65
  136.1 5.2 fusion.63
  141.3 5.2 fusion.22
  146.5 5.3 multiply_convert_fusion.2
  151.8 5.0 fusion.49
  156.9 5.0 fusion.53
  161.9 5.1 fusion.24
  166.9 5.3 fusion.23
  172.2 5.0 fusion.62
  177.3 5.0 fusion.61
  182.3 5.4 fusion.16
  187.7 5.8 multiply_bitcast_fusion.3
  197.0 4.3 broadcast.42.clone
  201.3 14.7 %dynamic_update_slice.6 = f32[2,1024,1024]{2,1,0:T(8,128)} dynamic-update-slice(f32[2,1024,1024]{2,1,0:T(8,128)} %broadcast.42.clone, f32[2,512,512]{2,1,0:T(8,128)S(1)} %copy.14, s32[]{:T(128)} %constant.11.clone.1, s32[]{:T(128)S(6)} %select_n.88, s32[]{:T(128)S(6)} %select_n.89) | dynamic-update-slice | bytes 4194308 | tf_op jit(solution)/shard_map/dynamic_update_slice | solution.py:83
  221.1 45.4 %collective-permute-done.2 = f32[2,1024,512]{2,1,0:T(8,128)S(1)} collective-permute-done((f32[2,1024,512]{2,1,0:T(8,128)S(1)}, f32[2,1024,512]{2,1,0:T(8,128)S(1)}, u32[]{:S(2)}, u32[]{:S(2)}) %collective-permute-start.2) | collective-permute-done | bytes 4194336 | tf_op jit(solution)/shard_map/ppermute | solution.py:18
  269.8 25.9 %collective-permute-done.3 = f32[2,512,512]{2,1,0:T(8,128)S(1)} collective-permute-done((f32[2,512,512]{2,1,0:T(8,128)S(1)}, f32[2,512,512]{2,1,0:T(8,128)S(1)}, u32[]{:S(2)}, u32[]{:S(2)}) %collective-permute-start.3) | collective-permute-done | bytes 2097184 | tf_op jit(solution)/shard_map/ppermute | solution.py:18
  296.4 17.3 %collective-permute-start.4 = (f32[2,512,512]{2,1,0:T(8,128)S(1)}, f32[2,512,512]{2,1,0:T(8,128)S(1)}, u32[]{:S(2)}, u32[]{:S(2)}) collective-permute-start(f32[2,512,512]{2,1,0:T(8,128)S(1)} %fusion.6), channel_id=1, source_target_pairs={{4,0},{8,4},{12,8},{16,12},{20,16},{24,20},{28,24},{5,1},{9,5},{13... | collective-permute-start | bytes 6291464 | tf_op jit(solution)/shard_map/ppermute | solution.py:18
  313.7 23.0 %collective-permute-done.4 = f32[2,512,512]{2,1,0:T(8,128)S(1)} collective-permute-done((f32[2,512,512]{2,1,0:T(8,128)S(1)}, f32[2,512,512]{2,1,0:T(8,128)S(1)}, u32[]{:S(2)}, u32[]{:S(2)}) %collective-permute-start.4) | collective-permute-done | bytes 2097184 | tf_op jit(solution)/shard_map/ppermute | solution.py:18
  339.0 47.9 %collective-permute-done.5 = f32[2,1024,512]{2,1,0:T(8,128)S(1)} collective-permute-done((f32[2,1024,512]{2,1,0:T(8,128)S(1)}, f32[2,1024,512]{2,1,0:T(8,128)S(1)}, u32[]{:S(2)}, u32[]{:S(2)}) %collective-permute-start.5) | collective-permute-done | bytes 4194336 | tf_op jit(solution)/shard_map/ppermute | solution.py:18
  395.5 5.0 fusion.58
  400.5 5.0 fusion.60
  405.5 5.1 fusion.30
  410.6 5.1 fusion.29
  415.7 5.0 fusion.59
  420.7 5.2 fusion.57
  425.9 5.2 fusion.14
  431.2 5.3 multiply_convert_fusion
  436.4 5.0 fusion.43
  441.5 5.0 fusion.47
  446.5 5.1 fusion.26
  451.6 5.5 fusion.25
  457.1 5.0 fusion.56
  462.1 5.0 fusion.55
  467.1 5.4 fusion.8
  472.6 5.8 multiply_bitcast_fusion.1
  482.8 4.3 broadcast.42
  487.2 15.2 %dynamic_update_slice.7 = f32[2,1024,1024]{2,1,0:T(8,128)} dynamic-update-slice(f32[2,1024,1024]{2,1,0:T(8,128)} %broadcast.42, f32[2,512,512]{2,1,0:T(8,128)} %copy.16, s32[]{:T(128)} %constant.11.clone.1, s32[]{:T(128)S(6)} %select_n.88, s32[]{:T(128)S(6)} %select_n.89) | dynamic-update-slice | bytes 4194308 | tf_op jit(solution)/shard_map/dynamic_update_slice | solution.py:83
  507.4 45.4 %collective-permute-done.6 = f32[2,1024,512]{2,1,0:T(8,128)S(1)} collective-permute-done((f32[2,1024,512]{2,1,0:T(8,128)S(1)}, f32[2,1024,512]{2,1,0:T(8,128)S(1)}, u32[]{:S(2)}, u32[]{:S(2)}) %collective-permute-start.6) | collective-permute-done | bytes 4194336 | tf_op jit(solution)/shard_map/ppermute | solution.py:18
  555.9 26.3 %collective-permute-done.7 = f32[2,512,512]{2,1,0:T(8,128)S(1)} collective-permute-done((f32[2,512,512]{2,1,0:T(8,128)S(1)}, f32[2,512,512]{2,1,0:T(8,128)S(1)}, u32[]{:S(2)}, u32[]{:S(2)}) %collective-permute-start.7) | collective-permute-done | bytes 2097184 | tf_op jit(solution)/shard_map/ppermute | solution.py:18
  (49 shorter events, 52.7 us)
Async XLA Ops:
  0.0 48.6 %collective-permute-start = (f32[2,512,512]{2,1,0:T(8,128)}, f32[2,512,512]{2,1,0:T(8,128)S(1)}, u32[]{:S(2)}, u32[]{:S(2)}) collective-permute-start(f32[2,512,512]{2,1,0:T(8,128)} %param.5), channel_id=1, source_target_pairs={{4,0},{8,4},{12,8},{16,12},{20,16},{24,20},{28,24},{5,1},{9,5},{13... | collective-permute-start | bytes 6291464 | tf_op jit(solution)/shard_map/ppermute | solution.py:18
  6.1 47.5 %copy-start.8 = (s32[1,1,1,2]{3,2,1,0:T(1,128)S(1)}, s32[1,1,1,2]{3,2,1,0:T(1,128)}, u32[]{:S(2)}) copy-start(s32[1,1,1,2]{3,2,1,0:T(1,128)} %param.8) | copy-start | bytes 28
  6.1 54.2 %copy-start.5 = (f32[1,1,1,512,512]{4,3,2,1,0:T(8,128)S(1)}, f32[1,1,1,512,512]{4,3,2,1,0:T(8,128)}, u32[]{:S(2)}) copy-start(f32[1,1,1,512,512]{4,3,2,1,0:T(8,128)} %param.7) | copy-start | bytes 3145732
  50.2 51.0 %collective-permute-start.1 = (f32[2,1024,512]{2,1,0:T(8,128)}, f32[2,1024,512]{2,1,0:T(8,128)}, u32[]{:S(2)}, u32[]{:S(2)}) collective-permute-start(f32[2,1024,512]{2,1,0:T(8,128)} %constant_dynamic-update-slice_fusion), channel_id=1, source_target_pairs={{1,0},{2,1},{3,2},{5,4},{6,5},{7,6},{9,8},{10,9},{11,10},{13,12},{... | collective-permute-start | bytes 12582920 | tf_op jit(solution)/shard_map/ppermute | solution.py:18
  64.1 123.6 %copy-start.2 = (f32[1,512,512]{1,2,0:T(8,128)}, f32[1,512,512]{1,2,0:T(8,128)S(1)}, u32[]{:S(2)}) copy-start(f32[1,512,512]{1,2,0:T(8,128)S(1)} %copy.22) | copy-start | bytes 3145732
  141.3 5.2 copy-start.6
  216.1 50.4 %copy-start.1 = (f32[2,1024,1024]{2,1,0:T(8,128)S(1)}, f32[2,1024,1024]{2,1,0:T(8,128)}, u32[]{:S(2)}) copy-start(f32[2,1024,1024]{2,1,0:T(8,128)} %dynamic_update_slice.6) | copy-start | bytes 25165828
  218.9 47.6 %collective-permute-start.2 = (f32[2,1024,512]{2,1,0:T(8,128)S(1)}, f32[2,1024,512]{2,1,0:T(8,128)S(1)}, u32[]{:S(2)}, u32[]{:S(2)}) collective-permute-start(f32[2,1024,512]{2,1,0:T(8,128)S(1)} %slice.117), channel_id=1, source_target_pairs={{0,1},{1,2},{2,3},{4,5},{5,6},{6,7},{8,9},{9,10},{10,11},{12,13},{... | collective-permute-start | bytes 12582920 | tf_op jit(solution)/shard_map/ppermute | solution.py:18
  267.5 28.1 %copy-start.4 = (f32[2,512,512]{2,1,0:T(8,128)S(1)}, f32[2,512,512]{2,1,0:T(8,128)}, u32[]{:S(2)}) copy-start(f32[2,512,512]{2,1,0:T(8,128)} %param.5) | copy-start | bytes 6291460
  267.7 27.9 %collective-permute-start.3 = (f32[2,512,512]{2,1,0:T(8,128)S(1)}, f32[2,512,512]{2,1,0:T(8,128)S(1)}, u32[]{:S(2)}, u32[]{:S(2)}) collective-permute-start(f32[2,512,512]{2,1,0:T(8,128)S(1)} %slice.119), channel_id=1, source_target_pairs={{0,4},{4,8},{8,12},{12,16},{16,20},{20,24},{24,28},{1,5},{5,9},{9,... | collective-permute-start | bytes 6291464 | tf_op jit(solution)/shard_map/ppermute | solution.py:18
  296.4 40.3 %collective-permute-start.4 = (f32[2,512,512]{2,1,0:T(8,128)S(1)}, f32[2,512,512]{2,1,0:T(8,128)S(1)}, u32[]{:S(2)}, u32[]{:S(2)}) collective-permute-start(f32[2,512,512]{2,1,0:T(8,128)S(1)} %fusion.6), channel_id=1, source_target_pairs={{4,0},{8,4},{12,8},{16,12},{20,16},{24,20},{28,24},{5,1},{9,5},{13... | collective-permute-start | bytes 6291464 | tf_op jit(solution)/shard_map/ppermute | solution.py:18
  337.1 49.8 %collective-permute-start.5 = (f32[2,1024,512]{2,1,0:T(8,128)S(1)}, f32[2,1024,512]{2,1,0:T(8,128)S(1)}, u32[]{:S(2)}, u32[]{:S(2)}) collective-permute-start(f32[2,1024,512]{2,1,0:T(8,128)S(1)} %pad_maximum_fusion), channel_id=1, source_target_pairs={{1,0},{2,1},{3,2},{5,4},{6,5},{7,6},{9,8},{10,9},{11,10},{13,12},{... | collective-permute-start | bytes 12582920 | tf_op jit(solution)/shard_map/ppermute | solution.py:18
  425.9 5.2 copy-start.7
  467.1 5.5 copy-start.3
  502.3 50.4 %copy-start = (f32[2,1024,1024]{2,1,0:T(8,128)S(1)}, f32[2,1024,1024]{2,1,0:T(8,128)}, u32[]{:S(2)}) copy-start(f32[2,1024,1024]{2,1,0:T(8,128)} %dynamic_update_slice.7) | copy-start | bytes 25165828
  505.2 47.6 %collective-permute-start.6 = (f32[2,1024,512]{2,1,0:T(8,128)S(1)}, f32[2,1024,512]{2,1,0:T(8,128)S(1)}, u32[]{:S(2)}, u32[]{:S(2)}) collective-permute-start(f32[2,1024,512]{2,1,0:T(8,128)S(1)} %slice.123), channel_id=1, source_target_pairs={{0,1},{1,2},{2,3},{4,5},{5,6},{6,7},{8,9},{9,10},{10,11},{12,13},{... | collective-permute-start | bytes 12582920 | tf_op jit(solution)/shard_map/ppermute | solution.py:18
  554.0 28.2 %collective-permute-start.7 = (f32[2,512,512]{2,1,0:T(8,128)S(1)}, f32[2,512,512]{2,1,0:T(8,128)S(1)}, u32[]{:S(2)}, u32[]{:S(2)}) collective-permute-start(f32[2,512,512]{2,1,0:T(8,128)S(1)} %slice.125), channel_id=1, source_target_pairs={{0,4},{4,8},{8,12},{12,16},{16,20},{20,24},{24,28},{1,5},{5,9},{9,... | collective-permute-start | bytes 6291464 | tf_op jit(solution)/shard_map/ppermute | solution.py:18
where the time goes:
time: 591 us; the launch traced here: 584 us
  waiting for transfers between devices  291 us (49%)
  matrix products  165 us (28%)
  local copies, waits for them, and re-layouts  65.5 us (11%)
  starting transfers between devices  34 us (6%)
  other arithmetic  20 us (3%)
  between operations  8.53 us (1%)
    ppermute x8, waiting for transfers between devices, shifted(): lax.ppermute(value, axis, [(source, source + steps) for source in range(l...  291 us
    dot_general x16, matrix products, left(): return jnp.einsum('ik,skj->sij', b, a, preferred_element_type=jnp.float32)  84 us
    dot_general x16, matrix products, right(): return jnp.einsum('swk,kj->swj', a, b, preferred_element_type=jnp.float32)  81.4 us
    ppermute x8, starting transfers between devices, shifted(): lax.ppermute(value, axis, [(source, source + steps) for source in range(l...  34 us
    dynamic_update_slice x2, local copies, waits for them, and re-layouts, add_piece(): return lax.dynamic_update_slice(region, piece, start)  29.9 us
  transfers between devices with their start and end apart: 8, of which 8 were waited for; matrix products, arithmetic and copies ran while one was open for 1% of the time, Pallas kernels for 0%

commit v1 on v0

v1 whole, which is shorter than its diff:
```python
import functools
import math

import jax
import jax.numpy as jnp
import numpy as np
from jax import lax
from jax.experimental import pallas as pl
from jax.experimental.pallas import tpu as pltpu
from jax.sharding import PartitionSpec as P

SWEEPS = 2
CHUNKS = 8

step_size = 0.5
floor_value = 0.05

MESH = pl.DeviceIdType.MESH
BF16 = jnp.bfloat16
F32 = jnp.float32


def dft_tables(width):
    index = np.arange(width)
    angle = (index[:, None] * index[None, :] % width) * (2.0 * math.pi / width)
    scale = 1.0 / math.sqrt(width)
    return (
        jnp.asarray((np.cos(angle) * scale).astype(np.float32).astype(BF16)),
        jnp.asarray((np.sin(angle) * scale).astype(np.float32).astype(BF16)),
    )


def dot(a, b):
    return jnp.dot(a, b, preferred_element_type=F32)


def iota(shape, axis):
    return lax.broadcasted_iota(jnp.int32, shape, axis)


def kernel(
    n_row, n_col, offs, meta, spec, pupil, amps, cosine, sine, out,
    below1, right1, diag1, give1, got1, own, down1, above1, tile2,
    below2, right2, diag2, give2, got2, down2, above2,
    pup, fwd_right, fwd_left, back_right, back_left, f1, f2, hot, left_dr, send, recv, meta_sem,
):
    width = spec.shape[1]
    size = width // CHUNKS
    r, c = lax.axis_index("row"), lax.axis_index("col")
    has_up, has_down = r > 0, r < n_row - 1
    has_left, has_right = c > 0, c < n_col - 1
    up = (lax.rem(r + n_row - 1, n_row), c)
    down = (lax.rem(r + 1, n_row), c)
    left = (r, lax.rem(c + n_col - 1, n_col))
    right = (r, lax.rem(c + 1, n_col))
    dr, dc = offs[0], offs[1]
    live = offs[2].astype(F32)

    def ds(k, block=size, base=0):
        return pl.ds(pl.multiple_of(base + k * block, 8), block)

    def flow(kind, src, dst, device):
        def copy(k):
            return pltpu.make_async_remote_copy(
                src_ref=src.at[:, ds(k), :], dst_ref=dst.at[:, ds(k), :],
                send_sem=send.at[kind, k], recv_sem=recv.at[kind, k],
                device_id=device, device_id_type=MESH,
            )
        return copy

    def each(body, count=CHUNKS):
        def step(k, carry):
            body(k)
            return carry
        lax.fori_loop(0, count, step, 0)

    neighbours = ((has_up, up), (has_down, down), (has_left, left), (has_right, right))
    barrier = pltpu.get_barrier_semaphore()
    for there, device in neighbours:
        @pl.when(there)
        def _():
            pl.semaphore_signal(barrier, inc=1, device_id=device, device_id_type=MESH)
    pl.semaphore_wait(barrier, sum(there.astype(jnp.int32) for there, _ in neighbours))

    up_flow = (flow(0, spec, below1, up), flow(5, tile2, below2, up))
    tile_flow = (flow(1, spec, right1, left), flow(6, tile2, right2, left))
    diag_flow = (flow(2, below1, diag1, left), flow(7, below2, diag2, left))
    give_flow = (flow(3, give1, got1, right), flow(8, give2, got2, right))
    down_flow = (flow(4, down1, above1, down), flow(9, down2, above2, down))

    def meta_copy():
        return pltpu.make_async_remote_copy(
            src_ref=meta, dst_ref=left_dr, send_sem=meta_sem.at[0], recv_sem=meta_sem.at[1],
            device_id=right, device_id_type=MESH,
        )

    @pl.when(has_right)
    def _():
        meta_copy().start()

    def first_sends(k):
        @pl.when(has_up)
        def _():
            up_flow[0](k).start()

        @pl.when(has_left)
        def _():
            tile_flow[0](k).start()

    each(first_sends)

    @pl.when(jnp.logical_not(has_down))
    def _():
        for ref in (below1, below2, diag1, diag2):
            ref[...] = jnp.zeros_like(ref)

    @pl.when(jnp.logical_not(has_right))
    def _():
        for ref in (right1, right2, diag1, diag2):
            ref[...] = jnp.zeros_like(ref)

    @pl.when(jnp.logical_not(has_left))
    def _():
        for ref in (got1, got2, left_dr):
            ref[...] = jnp.zeros_like(ref)

    @pl.when(jnp.logical_not(has_up))
    def _():
        for ref in (above1, above2):
            ref[...] = jnp.zeros_like(ref)

    block = 128
    shape = (block, width)

    def wrapped(value):
        return jnp.where(value >= width, value - width, value)

    def one_hot(mask):
        return jnp.where(mask, 1.0, 0.0).astype(BF16)

    def columns_of(i):
        at = iota(shape, 0) + i * block
        hot[0, ds(i, block)] = one_hot(iota(shape, 1) == wrapped(at + dr))
        hot[1, ds(i, block)] = one_hot(iota(shape, 1) == wrapped(at + dc))

    each(columns_of, width // block)

    def rows_hot(i, shift):
        return one_hot(iota(shape, 0) + i * block == wrapped(iota(shape, 1) + shift))

    def tables(i):
        top, low = ds(i, block), ds(i, block, width)
        near, far = pl.ds(0, width), pl.ds(width, width)

        def put(ref, cos, sin, top_sign, low_sign):
            ref[top, near] = cos.astype(BF16)
            ref[low, far] = cos.astype(BF16)
            ref[top, far] = (top_sign * sin).astype(BF16)
            ref[low, near] = (low_sign * sin).astype(BF16)

        hot_rows = rows_hot(i, dc)
        put(fwd_right, dot(hot_rows, cosine[...]), dot(hot_rows, sine[...]), 1.0, -1.0)
        hot_rows = rows_hot(i, dr)
        put(back_left, dot(hot_rows, cosine[...]), dot(hot_rows, sine[...]), 1.0, -1.0)
        cos, sin = cosine[ds(i, block)], sine[ds(i, block)]
        put(fwd_left, dot(cos, hot[0]), dot(sin, hot[0]), -1.0, 1.0)
        put(back_right, dot(cos, hot[1]), dot(sin, hot[1]), -1.0, 1.0)

    each(tables, width // block)

    def three(value):
        high = value.astype(BF16)
        rest = value - high.astype(F32)
        middle = rest.astype(BF16)
        return high, middle, (rest - middle.astype(F32)).astype(BF16)

    for plane in range(2):
        def pupil_columns(i):
            parts = three(pupil[plane, ds(i, block)])
            moved = [dot(part, hot[1]) for part in parts]
            f1[ds(i, block)] = moved[0].astype(BF16)
            f1[ds(i, block, width)] = moved[1].astype(BF16)
            f2[ds(i, block)] = moved[2].astype(BF16)

        each(pupil_columns, width // block)

        def pupil_rows(i):
            hot_rows = rows_hot(i, dr)
            high = dot(hot_rows, f1[0:width])
            middle = dot(hot_rows, f1[width : 2 * width])
            pup[plane, ds(i, block)] = high + middle + dot(hot_rows, f2[0:width])

        each(pupil_rows, width // block)

    def masks(k):
        row = iota((size, width), 0) + k * size
        return row, row < dr, iota((size, width), 1) < dc

    def window(k, tile, below, right_tile, diag):
        _, low, far = masks(k)
        rows = ds(k)
        planes = [
            jnp.where(
                far,
                jnp.where(low, diag[p, rows], right_tile[p, rows]),
                jnp.where(low, below[p, rows], tile[p, rows]),
            )
            for p in range(2)
        ]
        pr, pi = pup[0, rows], pup[1, rows]
        field_real = planes[0] * pr - planes[1] * pi
        field_imag = planes[0] * pi + planes[1] * pr
        both = jnp.concatenate([field_real, field_imag], axis=1).astype(BF16)
        first = dot(both, fwd_right[...])
        f1[rows] = first[:, :width].astype(BF16)
        f1[ds(k, size, width)] = first[:, width:].astype(BF16)

    def middle(i):
        rows, low = ds(i, block), ds(i, block, width)
        wave_real = dot(fwd_left[rows], f1[...])
        wave_imag = dot(fwd_left[low], f1[...])
        magnitude = jnp.sqrt(wave_real * wave_real + wave_imag * wave_imag)
        keep = 1.0 - amps[rows] / jnp.maximum(magnitude, floor_value)
        both = jnp.concatenate([wave_real * keep, wave_imag * keep], axis=1).astype(BF16)
        first = dot(both, back_right[...])
        f2[rows] = first[:, :width].astype(BF16)
        f2[low] = first[:, width:].astype(BF16)

    tiles = (spec, tile2, out)
    for sweep in range(SWEEPS):
        tile, following = tiles[sweep], tiles[sweep + 1]
        below, right_tile, diag = ((below1, right1, diag1), (below2, right2, diag2))[sweep]
        give, got, lower, above = ((give1, got1, down1, above1), (give2, got2, down2, above2))[sweep]

        def relay(k):
            @pl.when(has_down)
            def _():
                up_flow[sweep](k).wait_recv()

                @pl.when(has_left)
                def _():
                    diag_flow[sweep](k).start()

        def consume(k):
            @pl.when(has_right)
            def _():
                tile_flow[sweep](k).wait_recv()

                @pl.when(has_down)
                def _():
                    diag_flow[sweep](k).wait_recv()

            window(k, tile, below, right_tile, diag)

        relay(0)

        def gather(k):
            relay(k + 1)
            consume(k)

        each(gather, CHUNKS - 1)
        consume(CHUNKS - 1)
        each(middle, width // block)

        def piece(k):
            _, _, far = masks(k)
            rows = ds(k)
            back_real = dot(back_left[rows], f2[...])
            back_imag = dot(back_left[ds(k, size, width)], f2[...])
            pr, pi = pup[0, rows], pup[1, rows]
            grads = (
                (back_real * pr + back_imag * pi) * live,
                (back_imag * pr - back_real * pi) * live,
            )
            for p in range(2):
                give[p, rows] = jnp.where(far, grads[p], 0.0)
                own[p, rows] = jnp.where(far, 0.0, grads[p])

            @pl.when(has_right)
            def _():
                give_flow[sweep](k).start()

        each(piece)

        if sweep == 0:
            @pl.when(has_left)
            def _():
                meta_copy().wait_recv()

        def pass_down(k):
            row, low, _ = masks(k)
            rows = ds(k)

            @pl.when(has_left)
            def _():
                give_flow[sweep](k).wait_recv()

            left_low = row.astype(F32) < left_dr[0:1, :]
            for p in range(2):
                mine, theirs = own[p, rows], got[p, rows]
                lower[p, rows] = jnp.where(low, mine, 0.0) + jnp.where(left_low, theirs, 0.0)
                kept = jnp.where(low, 0.0, mine) + jnp.where(left_low, 0.0, theirs)
                following[p, rows] = tile[p, rows] - step_size * kept

            @pl.when(has_down)
            def _():
                down_flow[sweep](k).start()

        each(pass_down)

        def finish(k):
            rows = ds(k)

            @pl.when(has_up)
            def _():
                down_flow[sweep](k).wait_recv()

            for p in range(2):
                following[p, rows] = following[p, rows] - step_size * above[p, rows]
            if sweep + 1 < SWEEPS:
                @pl.when(has_up)
                def _():
                    up_flow[sweep + 1](k).start()

                @pl.when(has_left)
                def _():
                    tile_flow[sweep + 1](k).start()

        each(finish)

    @pl.when(has_right)
    def _():
        meta_copy().wait_send()

    def sent(k):
        for sweep in range(SWEEPS):
            @pl.when(has_up)
            def _():
                up_flow[sweep](k).wait_send()

            @pl.when(has_left)
            def _():
                tile_flow[sweep](k).wait_send()

                @pl.when(has_down)
                def _():
                    diag_flow[sweep](k).wait_send()

            @pl.when(has_right)
            def _():
                give_flow[sweep](k).wait_send()

            @pl.when(has_down)
            def _():
                down_flow[sweep](k).wait_send()

    each(sent)


def on_device(n_row, n_col, spectrum, pupil, amplitudes, offsets, counts):
    width = pupil.shape[1]
    amps = amplitudes[0, 0, 0]
    place = offsets[0, 0, 0]
    live = (counts[0, 0] > 0).astype(jnp.int32)
    offs = jnp.concatenate([place, live[None]])
    meta = jnp.broadcast_to(place[0].astype(F32), (8, width))
    cosine, sine = dft_tables(width)
    plane = pltpu.VMEM((2, width, width), F32)
    table = pltpu.VMEM((2 * width, 2 * width), BF16)
    stage = pltpu.VMEM((2 * width, width), BF16)
    vmem = pl.BlockSpec(memory_space=pltpu.VMEM)
    return pl.pallas_call(
        functools.partial(kernel, n_row, n_col),
        out_shape=jax.ShapeDtypeStruct(spectrum.shape, F32),
        in_specs=[pl.BlockSpec(memory_space=pltpu.SMEM)] + [vmem] * 6,
        out_specs=vmem,
        scratch_shapes=[plane] * 17
        + [table] * 4
        + [stage] * 2
        + [
            pltpu.VMEM((2, width, width), BF16),
            pltpu.VMEM((8, width), F32),
            pltpu.SemaphoreType.DMA((5 * SWEEPS, CHUNKS)),
            pltpu.SemaphoreType.DMA((5 * SWEEPS, CHUNKS)),
            pltpu.SemaphoreType.DMA((2,)),
        ],
        compiler_params=pltpu.CompilerParams(
            collective_id=0, has_side_effects=True, vmem_limit_bytes=66 * 1000 * 1000
        ),
    )(offs, meta, spectrum, pupil, amps, cosine, sine)


def solution(mesh):
    in_specs = (
        P(None, "row", "col"),
        P(),
        P("row", "col", None, None, None),
        P("row", "col", None, None),
        P("row", "col"),
    )
    return jax.shard_map(
        functools.partial(on_device, mesh.shape["row"], mesh.shape["col"]),
        mesh=mesh, in_specs=in_specs, out_specs=P(None, "row", "col"), check_vma=False,
    )
```

time: 591 us -> 241 us (0.41); the launches traced: 584 us -> 240 us
  waiting for transfers between devices: 291 us -> 0 us
  Pallas kernels: 0 us -> 234 us
  matrix products: 165 us -> 0 us
  local copies, waits for them, and re-layouts: 65.5 us -> 3.69 us
  starting transfers between devices: 34 us -> 0 us
  other arithmetic: 20 us -> 1.25 us
  between operations: 8.53 us -> 1.31 us
    ppermute x8 -> x0, waiting for transfers between devices: 291 us -> none  [shifted(): lax.ppermute(value, axis, [(source, source + steps) for source in range(l...]
    pallas_call x0 -> x1, Pallas kernels: none -> 234 us  [on_device(): pl.pallas_call(functools.partial(kernel, n_row, n_col), out_shape=jax.Sha...]
    dot_general x32 -> x0, matrix products: 165 us -> none  [the longest x16 84 us: left(): return jnp.einsum('ik,skj->sij', b, a, preferred_element_type=jnp.float32)]
    ppermute x8 -> x0, starting transfers between devices: 34 us -> none  [shifted(): lax.ppermute(value, axis, [(source, source + steps) for source in range(l...]
    dynamic_update_slice x2 -> x0, local copies, waits for them, and re-layouts: 29.9 us -> none  [add_piece(): return lax.dynamic_update_slice(region, piece, start)]
    another operation x4 -> x0, local copies, waits for them, and re-layouts: 15.1 us -> none
    slice x7 -> x0, local copies, waits for them, and re-layouts: 8.79 us -> none  [the longest x2 5.59 us: fold_back(): right = shifted(region[:, :, cols:], 'col', 1)]
    concatenate x3 -> x1, other arithmetic: 7.69 us -> 1.25 us  [on_device(): offs = jnp.concatenate([place, live[None]])]
  transfers between devices with their start and end apart: 8 -> 0, of which waited for: 8 -> 0; matrix products, arithmetic and copies ran while one was open for 1% -> 0% of each run, Pallas kernels for 0% -> 0%
where the time goes in v1:
time: 241 us; the launch traced here: 240 us
  Pallas kernels  234 us (97%)
  local copies, waits for them, and re-layouts  3.69 us (2%)
    pallas_call x1, Pallas kernels, on_device(): pl.pallas_call(functools.partial(kernel, n_row, n_col), out_shape=jax.Sha...  234 us

profile of v1, /device:TPU:25, one launch (start us, length us, event | category | flops | bytes accessed | tf_op | source)
XLA Modules:
  0.0 240.4 jit_solution(16716299396554353640)
XLA Ops:
  1.3 1.2 pad_add_fusion.offs
  2.5 0.6 broadcast_in_dim.11.meta
  3.2 234.2 %shard_map.73 = f32[2,512,512]{2,1,0:T(8,128)} custom-call(s32[3]{0:T(128)} %pad_add_fusion.offs, f32[8,512]{1,0:T(8,128)} %broadcast_in_dim.11.meta, f32[2,512,512]{2,1,0:T(8,128)} %spec.1, f32[2,512,512]{2,1,0:T(8,128)} %pupil.1, f32[512,512]{1,0:T(8,128)} %bitcast.5, bf16[512,512]{1,0:T(8,128)(2,1)} %constant.7.clone.cosine, ...), custom_call_target="tpu_custom_call" | custom-call | tf_op jit(solution)/shard_map/pallas_call | solution.py:372
  237.4 3.1 %copy.10 = f32[2,512,512]{2,1,0:T(8,128)} copy(f32[2,512,512]{2,1,0:T(8,128)} %shard_map.73) | data formatting | bytes 4194304

commit v2 on v1

--- a/solution.py
+++ b/solution.py
@@ -10,7 +10,8 @@
 from jax.sharding import PartitionSpec as P
 
 SWEEPS = 2
-CHUNKS = 8
+CHUNKS = 16
+LAG = 4
 
 step_size = 0.5
 floor_value = 0.05
@@ -39,10 +40,11 @@
 
 
 def kernel(
-    n_row, n_col, offs, meta, spec, pupil, amps, cosine, sine, out,
+    n_row, n_col, place, count, spec, pupil_in, amps_in, cosine_in, sine_in, out,
     below1, right1, diag1, give1, got1, own, down1, above1, tile2,
     below2, right2, diag2, give2, got2, down2, above2,
     pup, fwd_right, fwd_left, back_right, back_left, f1, f2, hot, left_dr, send, recv, meta_sem,
+    meta, pupil, amps, cosine, sine, load,
 ):
     width = spec.shape[1]
     size = width // CHUNKS
@@ -53,8 +55,17 @@
     down = (lax.rem(r + 1, n_row), c)
     left = (r, lax.rem(c + n_col - 1, n_col))
     right = (r, lax.rem(c + 1, n_col))
-    dr, dc = offs[0], offs[1]
-    live = offs[2].astype(F32)
+    dr, dc = place[0], place[1]
+    live = jnp.where(count[0] > 0, 1.0, 0.0)
+    loads = [
+        pltpu.make_async_copy(source, target, load.at[at])
+        for at, (source, target) in enumerate(
+            ((cosine_in, cosine), (sine_in, sine), (pupil_in, pupil), (amps_in, amps))
+        )
+    ]
+    for copy in loads:
+        copy.start()
+    meta[...] = jnp.zeros_like(meta) + dr.astype(F32)
 
     def ds(k, block=size, base=0):
         return pl.ds(pl.multiple_of(base + k * block, 8), block)
@@ -94,10 +105,6 @@
             device_id=right, device_id_type=MESH,
         )
 
-    @pl.when(has_right)
-    def _():
-        meta_copy().start()
-
     def first_sends(k):
         @pl.when(has_up)
         def _():
@@ -128,6 +135,10 @@
     def _():
         for ref in (above1, above2):
             ref[...] = jnp.zeros_like(ref)
+
+    @pl.when(has_right)
+    def _():
+        meta_copy().start()
 
     block = 128
     shape = (block, width)
@@ -166,6 +177,8 @@
         put(fwd_left, dot(cos, hot[0]), dot(sin, hot[0]), -1.0, 1.0)
         put(back_right, dot(cos, hot[1]), dot(sin, hot[1]), -1.0, 1.0)
 
+    for copy in loads:
+        copy.wait()
     each(tables, width // block)
 
     def three(value):
@@ -215,10 +228,12 @@
         f1[rows] = first[:, :width].astype(BF16)
         f1[ds(k, size, width)] = first[:, width:].astype(BF16)
 
+    wide = width // 2
+
     def middle(i):
-        rows, low = ds(i, block), ds(i, block, width)
-        wave_real = dot(fwd_left[rows], f1[...])
-        wave_imag = dot(fwd_left[low], f1[...])
+        rows, low = ds(i, wide), ds(i, wide, width)
+        wave = dot(jnp.concatenate([fwd_left[rows], fwd_left[low]], axis=0), f1[...])
+        wave_real, wave_imag = wave[:wide], wave[wide:]
         magnitude = jnp.sqrt(wave_real * wave_real + wave_imag * wave_imag)
         keep = 1.0 - amps[rows] / jnp.maximum(magnitude, floor_value)
         both = jnp.concatenate([wave_real * keep, wave_imag * keep], axis=1).astype(BF16)
@@ -260,13 +275,14 @@
 
         each(gather, CHUNKS - 1)
         consume(CHUNKS - 1)
-        each(middle, width // block)
+        each(middle, width // wide)
 
         def piece(k):
             _, _, far = masks(k)
             rows = ds(k)
-            back_real = dot(back_left[rows], f2[...])
-            back_imag = dot(back_left[ds(k, size, width)], f2[...])
+            low = ds(k, size, width)
+            back = dot(jnp.concatenate([back_left[rows], back_left[low]], axis=0), f2[...])
+            back_real, back_imag = back[:size], back[size:]
             pr, pi = pup[0, rows], pup[1, rows]
             grads = (
                 (back_real * pr + back_imag * pi) * live,
@@ -280,7 +296,7 @@
             def _():
                 give_flow[sweep](k).start()
 
-        each(piece)
+        each(piece, LAG)
 
         if sweep == 0:
             @pl.when(has_left)
@@ -306,7 +322,15 @@
             def _():
                 down_flow[sweep](k).start()
 
-        each(pass_down)
+        def both_ways(k):
+            piece(k + LAG)
+            pass_down(k)
+
+        def last_down(k):
+            pass_down(k + CHUNKS - LAG)
+
+        each(both_ways, CHUNKS - LAG)
+        each(last_down, LAG)
 
         def finish(k):
             rows = ds(k)
@@ -360,10 +384,8 @@
 def on_device(n_row, n_col, spectrum, pupil, amplitudes, offsets, counts):
     width = pupil.shape[1]
     amps = amplitudes[0, 0, 0]
-    place = offsets[0, 0, 0]
-    live = (counts[0, 0] > 0).astype(jnp.int32)
-    offs = jnp.concatenate([place, live[None]])
-    meta = jnp.broadcast_to(place[0].astype(F32), (8, width))
+    place = offsets.reshape(-1)
+    count = counts.reshape(-1)
     cosine, sine = dft_tables(width)
     plane = pltpu.VMEM((2, width, width), F32)
     table = pltpu.VMEM((2 * width, 2 * width), BF16)
@@ -372,7 +394,9 @@
     return pl.pallas_call(
         functools.partial(kernel, n_row, n_col),
         out_shape=jax.ShapeDtypeStruct(spectrum.shape, F32),
-        in_specs=[pl.BlockSpec(memory_space=pltpu.SMEM)] + [vmem] * 6,
+        in_specs=[pl.BlockSpec(memory_space=pltpu.SMEM)] * 2
+        + [vmem]
+        + [pl.BlockSpec(memory_space=pltpu.MemorySpace.HBM)] * 4,
         out_specs=vmem,
         scratch_shapes=[plane] * 17
         + [table] * 4
@@ -383,11 +407,17 @@
             pltpu.SemaphoreType.DMA((5 * SWEEPS, CHUNKS)),
             pltpu.SemaphoreType.DMA((5 * SWEEPS, CHUNKS)),
             pltpu.SemaphoreType.DMA((2,)),
+            pltpu.VMEM((8, width), F32),
+            plane,
+            pltpu.VMEM((width, width), F32),
+            pltpu.VMEM((width, width), BF16),
+            pltpu.VMEM((width, width), BF16),
+            pltpu.SemaphoreType.DMA((4,)),
         ],
         compiler_params=pltpu.CompilerParams(
             collective_id=0, has_side_effects=True, vmem_limit_bytes=66 * 1000 * 1000
         ),
-    )(offs, meta, spectrum, pupil, amps, cosine, sine)
+    )(place, count, spectrum, pupil, amps, cosine, sine)
 
 
 def solution(mesh):

time: 241 us -> 234 us (0.971)
  Pallas kernels: 234 us -> 230 us
    pallas_call x1, Pallas kernels: 234 us -> 230 us  [on_device(): pl.pallas_call(functools.partial(kernel, n_row, n_col), out_shape=jax.Sha...]
where the time goes in v2:
time: 234 us
  Pallas kernels  230 us (98%)
  local copies, waits for them, and re-layouts  3.08 us (1%)
    pallas_call x1, Pallas kernels, on_device(): pl.pallas_call(functools.partial(kernel, n_row, n_col), out_shape=jax.Sha...  230 us

profile of v2, /device:TPU:25, one launch (start us, length us, event | category | flops | bytes accessed | tf_op | source)
XLA Modules:
  0.0 233.9 jit_solution(8997554820890543655)
XLA Ops:
  0.7 230.2 %shard_map.73 = f32[2,512,512]{2,1,0:T(8,128)} custom-call(s32[2]{0:T(128)} %bitcast.5, s32[1]{0:T(128)} %bitcast.3.count, f32[2,512,512]{2,1,0:T(8,128)} %spec.1, f32[2,512,512]{2,1,0:T(8,128)} %pupil_in.1, f32[512,512]{1,0:T(8,128)} %bitcast.4, bf16[512,512]{1,0:T(8,128)(2,1)} %constant.4.clone.cosine_in, bf16[512,512]{1,0:T(8,128)(2,1)} %constant.5.clone.sine_in), custom_call_target="tpu_custom_call" | custom-call | tf_op jit(solution)/shard_map/pallas_call | solution.py:394
  230.8 3.1 %copy.10 = f32[2,512,512]{2,1,0:T(8,128)} copy(f32[2,512,512]{2,1,0:T(8,128)} %shard_map.73) | data formatting | bytes 4194304

commit v3 on v2

--- a/solution.py
+++ b/solution.py
@@ -41,8 +41,8 @@
 
 def kernel(
     n_row, n_col, place, count, spec, pupil_in, amps_in, cosine_in, sine_in, out,
-    below1, right1, diag1, give1, got1, own, down1, above1, tile2,
-    below2, right2, diag2, give2, got2, down2, above2,
+    below1, right1, mix1, give1, got1, own, down1, above1, tile2,
+    below2, right2, mix2, give2, got2, down2, above2,
     pup, fwd_right, fwd_left, back_right, back_left, f1, f2, hot, left_dr, send, recv, meta_sem,
     meta, pupil, amps, cosine, sine, load,
 ):
@@ -93,11 +93,10 @@
             pl.semaphore_signal(barrier, inc=1, device_id=device, device_id_type=MESH)
     pl.semaphore_wait(barrier, sum(there.astype(jnp.int32) for there, _ in neighbours))
 
-    up_flow = (flow(0, spec, below1, up), flow(5, tile2, below2, up))
-    tile_flow = (flow(1, spec, right1, left), flow(6, tile2, right2, left))
-    diag_flow = (flow(2, below1, diag1, left), flow(7, below2, diag2, left))
-    give_flow = (flow(3, give1, got1, right), flow(8, give2, got2, right))
-    down_flow = (flow(4, down1, above1, down), flow(9, down2, above2, down))
+    up_flow = (flow(0, spec, below1, up), flow(3, tile2, below2, up))
+    left_flow = (flow(1, mix1, right1, left), flow(2, mix2, right2, left))
+    give_flow = (flow(4, give1, got1, right), flow(5, give2, got2, right))
+    down_flow = (flow(6, down1, above1, down), flow(7, down2, above2, down))
 
     def meta_copy():
         return pltpu.make_async_remote_copy(
@@ -110,20 +109,16 @@
         def _():
             up_flow[0](k).start()
 
-        @pl.when(has_left)
-        def _():
-            tile_flow[0](k).start()
-
     each(first_sends)
 
     @pl.when(jnp.logical_not(has_down))
     def _():
-        for ref in (below1, below2, diag1, diag2):
+        for ref in (below1, below2):
             ref[...] = jnp.zeros_like(ref)
 
     @pl.when(jnp.logical_not(has_right))
     def _():
-        for ref in (right1, right2, diag1, diag2):
+        for ref in (right1, right2):
             ref[...] = jnp.zeros_like(ref)
 
     @pl.when(jnp.logical_not(has_left))
@@ -209,14 +204,12 @@
         row = iota((size, width), 0) + k * size
         return row, row < dr, iota((size, width), 1) < dc
 
-    def window(k, tile, below, right_tile, diag):
+    def window(k, tile, below, right_tile):
         _, low, far = masks(k)
         rows = ds(k)
         planes = [
             jnp.where(
-                far,
-                jnp.where(low, diag[p, rows], right_tile[p, rows]),
-                jnp.where(low, below[p, rows], tile[p, rows]),
+                far, right_tile[p, rows], jnp.where(low, below[p, rows], tile[p, rows])
             )
             for p in range(2)
         ]
@@ -244,7 +237,7 @@
     tiles = (spec, tile2, out)
     for sweep in range(SWEEPS):
         tile, following = tiles[sweep], tiles[sweep + 1]
-        below, right_tile, diag = ((below1, right1, diag1), (below2, right2, diag2))[sweep]
+        below, right_tile, mix = ((below1, right1, mix1), (below2, right2, mix2))[sweep]
         give, got, lower, above = ((give1, got1, down1, above1), (give2, got2, down2, above2))[sweep]
 
         def relay(k):
@@ -252,20 +245,26 @@
             def _():
                 up_flow[sweep](k).wait_recv()
 
-                @pl.when(has_left)
-                def _():
-                    diag_flow[sweep](k).start()
+            @pl.when(has_left)
+            def _():
+                rows = ds(k)
+                row, _, _ = masks(k)
+                left_low = row.astype(F32) < left_dr[0:1, :]
+                for p in range(2):
+                    mix[p, rows] = jnp.where(left_low, below[p, rows], tile[p, rows])
+                left_flow[sweep](k).start()
 
         def consume(k):
             @pl.when(has_right)
             def _():
-                tile_flow[sweep](k).wait_recv()
-
-                @pl.when(has_down)
-                def _():
-                    diag_flow[sweep](k).wait_recv()
-
-            window(k, tile, below, right_tile, diag)
+                left_flow[sweep](k).wait_recv()
+
+            window(k, tile, below, right_tile)
+
+        if sweep == 0:
+            @pl.when(has_left)
+            def _():
+                meta_copy().wait_recv()
 
         relay(0)
 
@@ -298,11 +297,6 @@
 
         each(piece, LAG)
 
-        if sweep == 0:
-            @pl.when(has_left)
-            def _():
-                meta_copy().wait_recv()
-
         def pass_down(k):
             row, low, _ = masks(k)
             rows = ds(k)
@@ -346,10 +340,6 @@
                 def _():
                     up_flow[sweep + 1](k).start()
 
-                @pl.when(has_left)
-                def _():
-                    tile_flow[sweep + 1](k).start()
-
         each(finish)
 
     @pl.when(has_right)
@@ -364,11 +354,7 @@
 
             @pl.when(has_left)
             def _():
-                tile_flow[sweep](k).wait_send()
-
-                @pl.when(has_down)
-                def _():
-                    diag_flow[sweep](k).wait_send()
+                left_flow[sweep](k).wait_send()
 
             @pl.when(has_right)
             def _():
@@ -404,8 +390,8 @@
         + [
             pltpu.VMEM((2, width, width), BF16),
             pltpu.VMEM((8, width), F32),
-            pltpu.SemaphoreType.DMA((5 * SWEEPS, CHUNKS)),
-            pltpu.SemaphoreType.DMA((5 * SWEEPS, CHUNKS)),
+            pltpu.SemaphoreType.DMA((4 * SWEEPS, CHUNKS)),
+            pltpu.SemaphoreType.DMA((4 * SWEEPS, CHUNKS)),
             pltpu.SemaphoreType.DMA((2,)),
             pltpu.VMEM((8, width), F32),
             plane,

time: 234 us -> 232 us (level)
  no operation moved by 1% of the time
where the time goes in v3:
time: 232 us
  Pallas kernels  228 us (98%)
  local copies, waits for them, and re-layouts  3.08 us (1%)
    pallas_call x1, Pallas kernels, on_device(): pl.pallas_call(functools.partial(kernel, n_row, n_col), out_shape=jax.Sha...  228 us

profile of v3, /device:TPU:25, one launch (start us, length us, event | category | flops | bytes accessed | tf_op | source)
XLA Modules:
  0.0 231.9 jit_solution(9318391037433648173)
XLA Ops:
  0.7 228.2 %shard_map.73 = f32[2,512,512]{2,1,0:T(8,128)} custom-call(s32[2]{0:T(128)} %bitcast.5, s32[1]{0:T(128)} %bitcast.3.count, f32[2,512,512]{2,1,0:T(8,128)} %spec.1, f32[2,512,512]{2,1,0:T(8,128)} %pupil_in.1, f32[512,512]{1,0:T(8,128)} %bitcast.4, bf16[512,512]{1,0:T(8,128)(2,1)} %constant.4.clone.cosine_in, bf16[512,512]{1,0:T(8,128)(2,1)} %constant.5.clone.sine_in), custom_call_target="tpu_custom_call" | custom-call | tf_op jit(solution)/shard_map/pallas_call | solution.py:380
  228.9 3.1 %copy.10 = f32[2,512,512]{2,1,0:T(8,128)} copy(f32[2,512,512]{2,1,0:T(8,128)} %shard_map.73) | data formatting | bytes 4194304
